TPU v7x, 32 devices: a whole 2x2x4 slice. The times are simulated.
32 devices in a mesh: group: 4 (over y, x), tm: 8 (over z, core).
Axes of the slice: x: 2, y: 2, z: 4, core: 2. Of those that a mesh axis runs over, the one named last changes fastest.
Arguments:
- precip: bfloat16 [4, 32, 1440, 720], P('group', 'tm'), may hold values from 0.099609375 to 4
- day_bins: int32 [32], replicated, may hold values from 0 to 15
- family_of: int32 [4], replicated, may hold values from 0 to 2
Outputs:
- day_mean: bfloat16 [4, 16, 1440, 720], P('group', None, 'tm')
- day_second: bfloat16 [4, 16, 1440, 720], P('group', None, 'tm')
- day_third: bfloat16 [4, 16, 1440, 720], P('group', None, 'tm')
- family_mean: bfloat16 [3, 16, 1440, 720], P(None, None, 'tm')
- anomaly_norm: float32 [4, 32], replicated
All inputs are finite; a program needn't handle non-finite values.
Results may differ from a plain program's by a relative error of at most 0.001.
The roundings to bfloat16 on the way count: a program that leaves them out, or rounds other values in their place, can miss the bound.
Values may be sent and summed in bfloat16 or wider, within the bound.
A program may use at most 192 MiB of HBM per device.

v0:
```python
import functools
import math

import jax
import jax.numpy as jnp
from jax import lax
from jax.experimental import pallas as pl
from jax.experimental.pallas import tpu as pltpu
from jax.sharding import PartitionSpec as P

DAYS = 16
FAM = 3
ROWS = 16
CHUNKS = 4


def lat_weight(count):
    rows_idx = jnp.arange(count, dtype=jnp.float32)
    return jnp.cos((-90.0 + (rows_idx + 0.5) * 180.0 / count) * (math.pi / 180.0))


def moments_kernel(limit, n_prev, bins, divisor, x_ref, *refs):
    refs = refs[n_prev:]
    mean_ref, second_ref, third_ref, piece_ref, norm_ref, acc, acc2, acc3 = refs
    steps, rows, lats = x_ref.shape
    days = acc.shape[0]
    step = pl.program_id(0)

    @pl.when(step == 0)
    def _():
        norm_ref[...] = jnp.zeros_like(norm_ref)

    acc[...] = jnp.zeros_like(acc)
    acc2[...] = jnp.zeros_like(acc2)
    acc3[...] = jnp.zeros_like(acc3)

    def add(t, carry):
        b = bins[t]
        acc[b] += x_ref[t].astype(jnp.float32)
        return carry

    lax.fori_loop(0, steps, add, 0, unroll=2)

    def mean(b, carry):
        m = acc[b] / divisor[b]
        acc[b] = m
        mean_ref[b] = m.astype(jnp.bfloat16)
        piece_ref[b] = m.astype(jnp.bfloat16)
        return carry

    lax.fori_loop(0, days, mean, 0)
    valid = lax.broadcasted_iota(jnp.int32, (rows, lats), 0) < limit - step * rows

    def moment(t, carry):
        b = bins[t]
        a = x_ref[t].astype(jnp.float32) - acc[b]
        q = a * a
        acc2[b] += q
        acc3[b] += q * a
        kept = jnp.where(valid, q, 0.0)
        folded = kept[0:8]
        for r in range(8, rows, 8):
            folded = folded + kept[r : r + 8]
        norm_ref[t] += folded
        return carry

    lax.fori_loop(0, steps, moment, 0, unroll=2)

    def close(b, carry):
        second_ref[b] = (acc2[b] / divisor[b]).astype(jnp.bfloat16)
        third_ref[b] = (acc3[b] / divisor[b]).astype(jnp.bfloat16)
        return carry

    lax.fori_loop(0, days, close, 0)


def moments(fields, bins, divisor, first, band, prev):
    steps, rows, lats = fields.shape
    grid = pl.cdiv(rows, ROWS)
    smem = pl.BlockSpec(memory_space=pltpu.SMEM)
    whole = pl.BlockSpec((DAYS, ROWS, lats), lambda i: (0, i + first, 0))
    piece = pl.BlockSpec((DAYS, ROWS, lats), lambda i: (0, i, 0))
    out = jax.ShapeDtypeStruct((DAYS, band, lats), jnp.bfloat16)
    return pl.pallas_call(
        functools.partial(moments_kernel, rows, len(prev)),
        grid=(grid,),
        in_specs=[smem, smem, pl.BlockSpec((steps, ROWS, lats), lambda i: (0, i, 0))]
        + [pl.BlockSpec(memory_space=pl.ANY)] * len(prev),
        out_specs=[whole] * 3 + [piece, pl.BlockSpec((steps, 8, lats), lambda i: (0, 0, 0))],
        out_shape=[out] * 3
        + [
            jax.ShapeDtypeStruct((DAYS, rows, lats), jnp.bfloat16),
            jax.ShapeDtypeStruct((steps, 8, lats), jnp.float32),
        ],
        scratch_shapes=[pltpu.VMEM((DAYS, ROWS, lats), jnp.float32)] * 3,
        input_output_aliases={3 + i: i for i in range(len(prev))},
        compiler_params=pltpu.CompilerParams(
            dimension_semantics=("arbitrary",), vmem_limit_bytes=40 * 2**20
        ),
        cost_estimate=pl.CostEstimate(
            flops=20 * fields.size, bytes_accessed=6 * fields.size, transcendentals=0
        ),
    )(bins, divisor, fields, *prev)


def family_kernel(hot, scale, m_ref, *refs):
    f_ref = refs[-1]
    models = m_ref.shape[0]

    def one(b, carry):
        fields = [m_ref[m, b].astype(jnp.float32) for m in range(models)]
        for f in range(FAM):
            total = fields[0] * hot[f, 0]
            for m in range(1, models):
                total = total + fields[m] * hot[f, m]
            f_ref[f, b] = (total * scale[f]).astype(jnp.bfloat16)
        return carry

    lax.fori_loop(0, m_ref.shape[1], one, 0, unroll=2)


def families(every, hot, scale, first, band, prev):
    models, days, rows, lats = every.shape
    smem = pl.BlockSpec(memory_space=pltpu.SMEM)
    return pl.pallas_call(
        family_kernel,
        grid=(pl.cdiv(rows, ROWS),),
        in_specs=[smem, smem, pl.BlockSpec((models, days, ROWS, lats), lambda i: (0, 0, i, 0))]
        + [pl.BlockSpec(memory_space=pl.ANY)] * len(prev),
        out_specs=pl.BlockSpec((FAM, days, ROWS, lats), lambda i: (0, 0, i + first, 0)),
        out_shape=jax.ShapeDtypeStruct((FAM, days, band, lats), jnp.bfloat16),
        input_output_aliases={3 + i: i for i in range(len(prev))},
        compiler_params=pltpu.CompilerParams(
            dimension_semantics=("arbitrary",), vmem_limit_bytes=40 * 2**20
        ),
        cost_estimate=pl.CostEstimate(
            flops=8 * every.size, bytes_accessed=4 * every.size, transcendentals=0
        ),
    )(hot, scale, every, *prev)


def local(parts, groups, precip, day_bins, family_of):
    _, own, lons, lats = precip.shape
    band = lons // parts
    steps = own * parts
    counts = jnp.sum(
        (day_bins[None, :] == jnp.arange(DAYS, dtype=jnp.int32)[:, None]).astype(jnp.float32), axis=1
    )
    divisor = jnp.maximum(counts, 1.0)
    hot = (family_of[None, :] == jnp.arange(FAM, dtype=jnp.int32)[:, None]).astype(jnp.float32)
    scale = 1.0 / jnp.maximum(jnp.sum(hot, axis=1), 1.0)
    weight = lat_weight(lats)
    total_weight = lons * jnp.sum(weight)

    blocks = -(-band // ROWS)
    chunks = min(CHUNKS, blocks)
    edges = [blocks * k // chunks for k in range(chunks + 1)]
    banded = precip.reshape(own, parts, band, lats)
    prev, fam_prev, norms = (), (), 0.0
    got, gathered = None, []
    for k in range(chunks):
        low, high = edges[k] * ROWS, min(edges[k + 1] * ROWS, band)
        sent = jnp.transpose(banded[:, :, low:high], (1, 0, 2, 3))
        if k == 1:
            sent, _ = lax.optimization_barrier((sent, got))
        if k >= 2:
            sent, got, gathered[k - 2] = lax.optimization_barrier((sent, got, gathered[k - 2]))
        got = lax.all_to_all(sent, "tm", split_axis=0, concat_axis=0)
        fields = got.reshape(steps, high - low, lats)
        *prev, piece, norm = moments(fields, day_bins, divisor, edges[k], band, tuple(prev))
        if k:
            piece, gathered[k - 1] = lax.optimization_barrier((piece, gathered[k - 1]))
        gathered.append(lax.all_gather(piece, "group", axis=0))
        norms = norms + jnp.sum(norm, axis=1)
    for k in range(chunks):
        fam_prev = (families(gathered[k], hot, scale, edges[k], band, fam_prev),)
    weighted = jnp.sum(norms * weight[None, :], axis=1)
    mine = jnp.arange(groups, dtype=jnp.int32)[:, None] == lax.axis_index("group")
    placed = jnp.where(mine, weighted[None, :], 0.0)
    anomaly_norm = jnp.sqrt(lax.psum(placed, ("group", "tm")) / total_weight)
    day_mean, day_second, day_third = (p[None] for p in prev)
    return (day_mean, day_second, day_third, fam_prev[0], anomaly_norm)


def solution(mesh):
    in_specs = (P("group", "tm", None, None), P(), P())
    out_specs = (
        P("group", None, "tm", None),
        P("group", None, "tm", None),
        P("group", None, "tm", None),
        P(None, None, "tm", None),
        P(),
    )
    body = functools.partial(local, mesh.shape["tm"], mesh.shape["group"])
    return jax.shard_map(body, mesh=mesh, in_specs=in_specs, out_specs=out_specs, check_vma=False)
```

profile of v0, /device:TPU:17, one launch (start us, length us, event | category | flops | bytes accessed | tf_op | source)
XLA Modules:
  0.0 398.8 jit_solution(1920842398466352369)
XLA Ops:
  7.2 12.5 %reshape.41 = bf16[4,8,180,720]{3,2,1,0:T(8,128)(2,1)} reshape(bf16[1,4,1440,720]{3,2,1,0:T(8,128)(2,1)} %param.3) | data formatting | bytes 16588800 | tf_op jit(solution)/shard_map/reshape | solution.py:158
  19.7 5.7 %slice_bitcast_fusion = (bf16[8,4,48,720]{3,2,0,1:T(8,128)(2,1)S(1)}, bf16[8,4,48,720]{3,2,0,1:T(8,128)(2,1)}, bf16[8,4,48,720]{3,2,0,1:T(8,128)(2,1)}) fusion(bf16[4,8,180,720]{3,2,1,0:T(8,128)(2,1)} %reshape.41), kind=kLoop, calls=%fused_computation | loop fusion | bytes 13271040 | tf_op jit(solution)/shard_map/transpose | solution.py:163
  25.4 1.6 copy.47
  27.0 5.5 %all-to-all-start = ((bf16[8,4,48,720]{3,2,1,0:T(8,128)(2,1)}), bf16[8,4,48,720]{3,2,1,0:T(8,128)(2,1)S(1)}, u32[]{:S(2)}, u32[]{:S(2)}) async-start(bf16[8,4,48,720]{3,2,1,0:T(8,128)(2,1)} %copy.47), calls=%async_computation | async-start | bytes 4718592 | tf_op jit(solution)/shard_map/all_to_all | solution.py:168
  32.5 0.1 convert_reduce_fusion
  32.6 50.7 %all-to-all-done = bf16[8,4,48,720]{3,2,1,0:T(8,128)(2,1)S(1)} async-done(((bf16[8,4,48,720]{3,2,1,0:T(8,128)(2,1)}), bf16[8,4,48,720]{3,2,1,0:T(8,128)(2,1)S(1)}, u32[]{:S(2)}, u32[]{:S(2)}) %all-to-all-start) | async-done | bytes 2211872 | tf_op jit(solution)/shard_map/all_to_all | solution.py:168
  83.3 6.0 %shard_map.74 = (bf16[16,180,720]{2,1,0:T(8,128)(2,1)S(1)}, bf16[16,180,720]{2,1,0:T(8,128)(2,1)S(1)}, bf16[16,180,720]{2,1,0:T(8,128)(2,1)}, bf16[16,48,720]{2,1,0:T(8,128)(2,1)}, f32[32,8,720]{2,1,0:T(8,128)S(1)}) custom-call(s32[32]{0:T(128)S(1)} %copy-done.17, f32[16]{0:T(128)S(1)} %broadcast_maximum_fusion.divisor, bf16[32,48,720]{2,1,0:T(8,128)(2,1)S(1)} %bitcast.34), custom_call_target="tpu_custom_call" | custom-call | flops 22118400 | bytes 6635520 | tf_op jit(solution)/shard_map/pallas_call | solution.py:84
  89.3 2.1 copy-done
  91.5 2.1 copy-done.4
  93.6 0.0 all-gather.9.cloned.1.call-update
  93.6 0.0 all-gather.11.cloned.1.call-start
  93.7 0.0 slice-start.1
  93.7 2.0 copy.48
  95.7 57.3 %all_to_all.20 = bf16[8,4,48,720]{3,2,1,0:T(8,128)(2,1)S(1)} all-to-all(bf16[8,4,48,720]{3,2,1,0:T(8,128)(2,1)S(1)} %copy.48), channel_id=1, replica_groups=mesh['group'=4,'tm'=8] {'tm'}, dimensions={0} | all-to-all | bytes 4423680 | tf_op jit(solution)/shard_map/all_to_all | solution.py:168
  153.0 6.1 %shard_map.75 = (bf16[16,180,720]{2,1,0:T(8,128)(2,1)S(1)}, bf16[16,180,720]{2,1,0:T(8,128)(2,1)S(1)}, bf16[16,180,720]{2,1,0:T(8,128)(2,1)}, bf16[16,48,720]{2,1,0:T(8,128)(2,1)}, f32[32,8,720]{2,1,0:T(8,128)S(1)}) custom-call(s32[32]{0:T(128)S(1)} %copy-done.17, ...), custom_call_target="tpu_custom_call", output_to_operand_aliasing={{0}: (3, {}), {1}: (4, {}), {2}: (5, {})} | custom-call | flops 22118400 | bytes 6635520 | tf_op jit(solution)/shard_map/pallas_call | solution.py:84
  159.1 2.1 copy-done.1
  161.2 2.1 copy-done.6
  163.3 0.0 all-gather.11.cloned.1.call-update
  163.4 0.0 all-gather.13.cloned.1.call-start
  163.4 0.0 slice-start.3
  163.4 2.0 copy.49
  165.5 57.4 %all_to_all.21 = bf16[8,4,48,720]{3,2,1,0:T(8,128)(2,1)S(1)} all-to-all(bf16[8,4,48,720]{3,2,1,0:T(8,128)(2,1)S(1)} %copy.49), channel_id=1, replica_groups=mesh['group'=4,'tm'=8] {'tm'}, dimensions={0} | all-to-all | bytes 4423680 | tf_op jit(solution)/shard_map/all_to_all | solution.py:168
  222.8 6.1 %shard_map.76 = (bf16[16,180,720]{2,1,0:T(8,128)(2,1)S(1)}, bf16[16,180,720]{2,1,0:T(8,128)(2,1)S(1)}, bf16[16,180,720]{2,1,0:T(8,128)(2,1)}, bf16[16,48,720]{2,1,0:T(8,128)(2,1)}, f32[32,8,720]{2,1,0:T(8,128)S(1)}) custom-call(s32[32]{0:T(128)S(1)} %copy-done.17, ...), custom_call_target="tpu_custom_call", output_to_operand_aliasing={{0}: (3, {}), {1}: (4, {}), {2}: (5, {})} | custom-call | flops 22118400 | bytes 6635520 | tf_op jit(solution)/shard_map/pallas_call | solution.py:84
  228.9 2.2 copy-done.2
  231.1 2.1 copy-done.8
  233.2 0.9 copy-done.13
  234.1 0.0 all-gather.13.cloned.1.call-update
  234.1 0.0 all-gather.15.cloned.1.call-start
  234.2 0.0 slice-start.4
  234.2 1.8 slice_bitcast_fusion.3
  236.0 0.0 slice-start.5
  236.0 1.4 copy.50
  237.4 44.9 %all_to_all.22 = bf16[8,4,36,720]{3,1,2,0:T(4,128)(2,1)S(1)} all-to-all(bf16[8,4,36,720]{3,1,2,0:T(4,128)(2,1)S(1)} %copy.50), channel_id=1, replica_groups=mesh['group'=4,'tm'=8] {'tm'}, dimensions={0} | all-to-all | bytes 3317760 | tf_op jit(solution)/shard_map/all_to_all | solution.py:168
  282.3 0.3 copy.51
  282.6 0.0 copy-start.18
  282.6 5.9 %shard_map.77 = (bf16[16,180,720]{2,1,0:T(8,128)(2,1)S(1)}, bf16[16,180,720]{2,1,0:T(8,128)(2,1)S(1)}, bf16[16,180,720]{2,1,0:T(8,128)(2,1)}, bf16[16,36,720]{2,1,0:T(8,128)(2,1)S(1)}, f32[32,8,720]{2,1,0:T(8,128)S(1)}) custom-call(s32[32]{0:T(128)S(1)} %copy-done.17, ...), custom_call_target="tpu_custom_call", output_to_operand_aliasing={{0}: (3, {}), {1}: (4, {}), {2}: (5, {})} | custom-call | flops 16588800 | bytes 4976640 | tf_op jit(solution)/shard_map/pallas_call | solution.py:84
  288.6 2.1 copy-done.3
  290.7 2.2 copy-done.9
  292.8 0.9 copy-done.15
  293.7 1.1 copy.52
  294.8 0.0 all-gather.15.cloned.1.call-update
  294.8 0.7 fusion.1
  296.2 0.1 fusion.2
  296.4 0.2 reduce_sum.74
  296.6 0.2 reduce_sum.75
  296.8 2.3 copy-done.10
  299.1 4.5 %shard_map.78.refs_0_ = bf16[3,16,180,720]{3,2,1,0:T(8,128)(2,1)} custom-call(f32[3,4]{1,0:T(4,128)S(1)} %fusion.hot, f32[3]{0:T(128)S(1)} %maximum_divide_fusion.scale, bf16[4,16,48,720]{3,2,1,0:T(8,128)(2,1)S(1)} %bitcast.38), custom_call_target="tpu_custom_call" | custom-call | flops 17694720 | bytes 8847360 | tf_op jit(solution)/shard_map/pallas_call | solution.py:125
  303.6 0.2 reduce_sum.76
  303.8 2.7 copy-done.11
  306.5 4.5 %shard_map.79.refs_0_ = bf16[3,16,180,720]{3,2,1,0:T(8,128)(2,1)} custom-call(f32[3,4]{1,0:T(4,128)S(1)} %fusion.hot, f32[3]{0:T(128)S(1)} %maximum_divide_fusion.scale, bf16[4,16,48,720]{3,2,1,0:T(8,128)(2,1)S(1)} %bitcast.39, bf16[3,16,180,720]{3,2,1,0:T(8,128)(2,1)} %shard_map.78.refs_0_), custom_call_target="tpu_custom_call", output_to_operand_aliasing={{}: (3, {})} | custom-call | flops 17694720 | bytes 8847360 | tf_op jit(solution)/shard_map/pallas_call | solution.py:125
  311.0 0.2 reduce_sum.77
  311.2 0.0 slice-start.9
  311.3 5.4 %copy.54 = bf16[1,16,180,720]{3,1,2,0:T(8,128)(2,1)} copy(bf16[1,16,180,720]{3,2,1,0:T(8,128)(2,1)} %bitcast.27) | data formatting | bytes 8294400
  316.7 2.9 copy.55
  319.6 2.9 copy.56
  322.6 0.1 multiply_reduce_fusion
  322.7 0.1 broadcast_select_fusion
  322.8 40.7 %psum.7 = f32[4,32]{1,0:T(4,128)S(1)} all-reduce(f32[4,32]{1,0:T(4,128)S(1)} %broadcast_select_fusion), channel_id=1, replica_groups=mesh['group'=4,'tm'=8] {'group','tm'}, use_global_device_ids=true, to_apply=%region_7.0 | all-reduce | flops 128 | bytes 1024 | tf_op jit(solution)/shard_map/psum | solution.py:180
  363.5 0.6 divide_sqrt_fusion
  364.1 2.3 copy-done.12
  366.5 4.5 %shard_map.80.refs_0_ = bf16[3,16,180,720]{3,2,1,0:T(8,128)(2,1)} custom-call(f32[3,4]{1,0:T(4,128)S(1)} %fusion.hot, f32[3]{0:T(128)S(1)} %maximum_divide_fusion.scale, bf16[4,16,48,720]{3,2,1,0:T(8,128)(2,1)S(1)} %bitcast.40, bf16[3,16,180,720]{3,2,1,0:T(8,128)(2,1)} %shard_map.79.refs_0_), custom_call_target="tpu_custom_call", output_to_operand_aliasing={{}: (3, {})} | custom-call | flops 17694720 | bytes 8847360 | tf_op jit(solution)/shard_map/pallas_call | solution.py:125
  371.0 4.0 copy.53
  374.9 4.4 %shard_map.81 = bf16[3,16,180,720]{3,2,1,0:T(8,128)(2,1)} custom-call(f32[3,4]{1,0:T(4,128)S(1)} %fusion.hot, f32[3]{0:T(128)S(1)} %maximum_divide_fusion.scale, bf16[4,16,36,720]{3,2,1,0:T(8,128)(2,1)S(1)} %bitcast.33, bf16[3,16,180,720]{3,2,1,0:T(8,128)(2,1)} %shard_map.80.refs_0_), custom_call_target="tpu_custom_call", output_to_operand_aliasing={{}: (3, {})} | custom-call | flops 13271040 | bytes 6635520 | tf_op jit(solution)/shard_map/pallas_call | solution.py:125
  379.3 13.0 %copy.57 = bf16[3,16,180,720]{3,1,2,0:T(8,128)(2,1)} copy(bf16[3,16,180,720]{3,2,1,0:T(8,128)(2,1)} %shard_map.81) | data formatting | bytes 24883200
  (59 shorter events, 0.2 us)
Async XLA Ops:
  25.4 7.1 %copy-start.17 = (s32[32]{0:T(128)S(1)}, s32[32]{0:T(128)}, u32[]{:S(2)}) copy-start(s32[32]{0:T(128)} %bins.7) | copy-start | bytes 388
  27.0 56.3 %all-to-all-start = ((bf16[8,4,48,720]{3,2,1,0:T(8,128)(2,1)}), bf16[8,4,48,720]{3,2,1,0:T(8,128)(2,1)S(1)}, u32[]{:S(2)}, u32[]{:S(2)}) async-start(bf16[8,4,48,720]{3,2,1,0:T(8,128)(2,1)} %copy.47), calls=%async_computation | async-start | bytes 4718592 | tf_op jit(solution)/shard_map/all_to_all | solution.py:168
  32.5 130.8 %all-gather.9.cloned.1.call-start = ((), (), s32[]{:S(2)}) async-start(), calls=%async_computation.4 | async-start | bytes 5898240 | tf_op jit(solution)/shard_map/all_gather | solution.py:173
  89.3 2.1 copy-start
  91.5 2.2 copy-start.4
  93.6 59.4 %slice-start = ((s8[4521984]{0:T(1024)(128)(4,1)}), s8[327680]{0:T(1024)(128)(4,1)S(1)}, s32[]{:S(2)}) async-start(s8[4521984]{0:T(1024)(128)(4,1)} %bitcast.21), calls=%async_computation.8 | async-start | bytes 655360
  93.6 140.5 %all-gather.11.cloned.1.call-start = ((), (), s32[]{:S(2)}) async-start(), calls=%async_computation.5 | async-start | bytes 5898240 | tf_op jit(solution)/shard_map/all_gather | solution.py:173
  93.7 59.3 %slice-start.1 = ((s8[4521984]{0:T(1024)(128)(4,1)}), s8[4194304]{0:T(1024)(128)(4,1)S(1)}, s32[]{:S(2)}) async-start(s8[4521984]{0:T(1024)(128)(4,1)} %bitcast.21), calls=%async_computation.9 | async-start | bytes 8388608
  93.7 59.3 %copy-start.5 = (bf16[16,180,720]{2,1,0:T(8,128)(2,1)S(1)}, bf16[16,180,720]{2,1,0:T(8,128)(2,1)}, u32[]{:S(2)}) copy-start(bf16[16,180,720]{2,1,0:T(8,128)(2,1)} %copy-done.4) | copy-start | bytes 12441604
  159.1 2.1 copy-start.1
  161.2 2.1 copy-start.6
  163.3 59.5 %slice-start.2 = ((s8[4521984]{0:T(1024)(128)(4,1)}), s8[327680]{0:T(1024)(128)(4,1)S(1)}, s32[]{:S(2)}) async-start(s8[4521984]{0:T(1024)(128)(4,1)} %bitcast.23), calls=%async_computation.10 | async-start | bytes 655360
  163.4 130.4 %all-gather.13.cloned.1.call-start = ((), (), s32[]{:S(2)}) async-start(), calls=%async_computation.6 | async-start | bytes 5898240 | tf_op jit(solution)/shard_map/all_gather | solution.py:173
  163.4 59.4 %slice-start.3 = ((s8[4521984]{0:T(1024)(128)(4,1)}), s8[4194304]{0:T(1024)(128)(4,1)S(1)}, s32[]{:S(2)}) async-start(s8[4521984]{0:T(1024)(128)(4,1)} %bitcast.23), calls=%async_computation.11 | async-start | bytes 8388608
  163.4 59.4 %copy-start.7 = (bf16[16,180,720]{2,1,0:T(8,128)(2,1)S(1)}, bf16[16,180,720]{2,1,0:T(8,128)(2,1)}, u32[]{:S(2)}) copy-start(bf16[16,180,720]{2,1,0:T(8,128)(2,1)} %copy-done.6) | copy-start | bytes 12441604
  228.9 2.2 copy-start.2
  231.1 2.1 copy-start.8
  233.2 0.9 copy-start.13
  234.1 136.8 %all-gather.15.cloned.1.call-start = ((), (), s32[]{:S(2)}) async-start(), calls=%async_computation.7 | async-start | bytes 4423680 | tf_op jit(solution)/shard_map/all_gather | solution.py:173
  234.2 48.4 %slice-start.4 = ((s8[4521984]{0:T(1024)(128)(4,1)}), s8[4194304]{0:T(1024)(128)(4,1)S(1)}, s32[]{:S(2)}) async-start(s8[4521984]{0:T(1024)(128)(4,1)} %bitcast.25), calls=%async_computation.12 | async-start | bytes 8388608
  234.2 48.4 %slice-start.6 = ((s8[4521984]{0:T(1024)(128)(4,1)}), s8[4194304]{0:T(1024)(128)(4,1)S(1)}, s32[]{:S(2)}) async-start(s8[4521984]{0:T(1024)(128)(4,1)} %bitcast.28), calls=%async_computation.14 | async-start | bytes 8388608
  236.0 46.5 %slice-start.5 = ((s8[4521984]{0:T(1024)(128)(4,1)}), s8[327680]{0:T(1024)(128)(4,1)S(1)}, s32[]{:S(2)}) async-start(s8[4521984]{0:T(1024)(128)(4,1)} %bitcast.25), calls=%async_computation.13 | async-start | bytes 655360
  236.0 46.5 %slice-start.7 = ((s8[4521984]{0:T(1024)(128)(4,1)}), s8[327680]{0:T(1024)(128)(4,1)S(1)}, s32[]{:S(2)}) async-start(s8[4521984]{0:T(1024)(128)(4,1)} %bitcast.28), calls=%async_computation.15 | async-start | bytes 655360
  282.6 13.6 %copy-start.18 = (s32[4]{0:T(128)S(1)}, s32[4]{0:T(128)}, u32[]{:S(2)}) copy-start(s32[4]{0:T(128)} %param.5) | copy-start | bytes 52
  288.6 2.1 copy-start.3
  290.7 2.2 copy-start.9
  292.8 0.9 copy-start.15
  296.8 2.3 copy-start.10
  299.1 4.5 %copy-start.14 = (f32[32,8,720]{2,1,0:T(8,128)S(1)}, f32[32,8,720]{2,1,0:T(8,128)}, u32[]{:S(2)}) copy-start(f32[32,8,720]{2,1,0:T(8,128)} %copy-done.13) | copy-start | bytes 2211844
  303.8 2.7 copy-start.11
  306.5 4.5 %copy-start.16 = (f32[32,8,720]{2,1,0:T(8,128)S(1)}, f32[32,8,720]{2,1,0:T(8,128)}, u32[]{:S(2)}) copy-start(f32[32,8,720]{2,1,0:T(8,128)} %copy-done.15) | copy-start | bytes 2211844
  311.0 5.6 %slice-start.8 = ((s8[4521984]{0:T(1024)(128)(4,1)}), s8[327680]{0:T(1024)(128)(4,1)S(1)}, s32[]{:S(2)}) async-start(s8[4521984]{0:T(1024)(128)(4,1)} %bitcast.30), calls=%async_computation.16 | async-start | bytes 655360
  311.2 5.4 %slice-start.9 = ((s8[4521984]{0:T(1024)(128)(4,1)}), s8[4194304]{0:T(1024)(128)(4,1)S(1)}, s32[]{:S(2)}) async-start(s8[4521984]{0:T(1024)(128)(4,1)} %bitcast.30), calls=%async_computation.17 | async-start | bytes 8388608
  311.3 8.4 %slice-start.10 = ((s8[4521984]{0:T(1024)(128)(4,1)}), s8[4194304]{0:T(1024)(128)(4,1)S(1)}, s32[]{:S(2)}) async-start(s8[4521984]{0:T(1024)(128)(4,1)} %bitcast.41), calls=%async_computation.18 | async-start | bytes 8388608
  316.7 3.0 slice-start.11
  364.1 2.3 copy-start.12
Sparse Core Ops, SparseCore 0:
  93.8 58.7 all-gather.8
  163.5 58.8 all-gather.10
  234.2 58.8 all-gather.12
  294.9 49.3 all-gather.14
where the time goes:
time: 403 us; the launch traced here: 399 us
  blocking collectives  200 us (50%)
  local copies, waits for them, and re-layouts  83 us (21%)
  waiting for transfers between devices  50.7 us (13%)
  Pallas kernels  42 us (10%)
  between operations  14.7 us (4%)
  starting transfers between devices  5.61 us (1%)
    all_to_all x3, blocking collectives, local(): got = lax.all_to_all(sent, 'tm', split_axis=0, concat_axis=0)  159 us
    all_to_all x1, waiting for transfers between devices, local(): got = lax.all_to_all(sent, 'tm', split_axis=0, concat_axis=0)  50.7 us
    unnamed x66, local copies, waits for them, and re-layouts  50.6 us
    psum x1, blocking collectives, local(): anomaly_norm = jnp.sqrt(lax.psum(placed, ('group', 'tm')) / total_weight)  40.7 us
    pallas_call x4, Pallas kernels, moments(): pl.pallas_call(functools.partial(moments_kernel, rows, len(prev)), grid=(...  24.1 us
    pallas_call x4, Pallas kernels, families(): pl.pallas_call(family_kernel, grid=(pl.cdiv(rows, ROWS),), in_specs=[smem...  17.9 us
    reshape x1, local copies, waits for them, and re-layouts, local(): banded = precip.reshape(own, parts, band, lats)  12.5 us
    transpose x3, local copies, waits for them, and re-layouts, local(): sent = jnp.transpose(banded[:, :, low:high], (1, 0, 2, 3))  9.18 us
  transfers between devices with their start and end apart: 5, of which 1 were waited for; matrix products, arithmetic and copies ran while one was open for 5% of the time, Pallas kernels for 8%

commit v1 on v0

v1 whole, which is shorter than its diff:
```python
import functools
import math

import jax
import jax.numpy as jnp
from jax import lax
from jax.experimental import pallas as pl
from jax.experimental.pallas import tpu as pltpu
from jax.sharding import PartitionSpec as P

DAYS = 16
FAM = 3
UNIT = 8
CHUNK = 16
WINDOW = 2
MESH = pl.DeviceIdType.MESH
F32 = jnp.float32
BF16 = jnp.bfloat16


def lat_weight(count):
    rows_idx = jnp.arange(count, dtype=F32)
    return jnp.cos((-90.0 + (rows_idx + 0.5) * 180.0 / count) * (math.pi / 180.0))


def partner(index, k, count):
    if count & (count - 1) == 0:
        return lax.bitwise_xor(index, k)
    return lax.rem(index + k, count)


def sender(index, k, count):
    if count & (count - 1) == 0:
        return lax.bitwise_xor(index, k)
    return lax.rem(index + count - k, count)


def lane_tiles(lats):
    return [(low, min(128, lats - low)) for low in range(0, lats, 128)]


def fused_kernel(
    parts, groups, band, lons, chunks,
    bins, prev, last, inverse, hot, scale, weight, x_ref,
    mean_ref, second_ref, third_ref, family_ref, norm_ref,
    land, slots, run, run2, run3, center, square, nvec, nland, gland,
    own_sem, z_send, z_recv, m_send, m_recv, n_send, n_recv, g_send, g_recv,
):
    steps, span, lats = land.shape
    own = steps // parts
    me, group = lax.axis_index("tm"), lax.axis_index("group")
    relay = groups == 4
    links = (1, 2) if relay else tuple(range(1, groups))
    tiles = lane_tiles(lats)

    barrier = pltpu.get_barrier_semaphore()
    for k in range(1, parts):
        pl.semaphore_signal(barrier, 1, device_id={"tm": partner(me, k, parts)}, device_id_type=MESH)
    for k in range(1, groups):
        pl.semaphore_signal(barrier, 1, device_id={"group": partner(group, k, groups)}, device_id_type=MESH)
    pl.semaphore_wait(barrier, parts + groups - 2)

    def first_row(part):
        low = jnp.minimum(part * band // UNIT * UNIT, lons - span)
        return pl.multiple_of(low, UNIT)

    def z_copy(c, start, rows, k):
        to = partner(me, k, parts)
        return pltpu.make_async_remote_copy(
            src_ref=x_ref.at[:, pl.ds(pl.multiple_of(first_row(to) + start, UNIT), rows)],
            dst_ref=land.at[pl.ds(me * own, own), pl.ds(start, rows)],
            send_sem=z_send.at[c, k - 1],
            recv_sem=z_recv.at[c, k - 1],
            device_id={"tm": to},
            device_id_type=MESH,
        )

    def z_start(c, start, rows):
        for k in range(1, parts):
            z_copy(c, start, rows, k).start()

    own_copy = pltpu.make_async_copy(
        x_ref.at[:, pl.ds(first_row(me), span)], land.at[pl.ds(me * own, own)], own_sem.at[0]
    )
    for c in range(min(WINDOW, len(chunks))):
        z_start(c, *chunks[c])
    own_copy.start()

    zeros = jnp.zeros((UNIT, lats), F32)
    run[steps] = zeros
    run2[steps] = zeros
    run3[steps] = zeros
    square[...] = jnp.zeros_like(square)
    offset = me * band - first_row(me)

    def spread(values, base, out):
        for low, width in tiles:
            part = values[:, :, low : low + width]
            out[pl.ds(base, UNIT), :, low : low + width] = jnp.swapaxes(part, 0, 1).astype(BF16)

    def unit(base):
        def add(t, carry):
            x = land[t, pl.ds(base, UNIT), :].astype(F32)
            run[t] = run[prev[t]] + x
            return carry

        lax.fori_loop(0, steps, add, 0, unroll=4)

        def mean(b, carry):
            center[b] = run[last[b]] * inverse[b]
            return carry

        lax.fori_loop(0, DAYS, mean, 0, unroll=2)
        spread(center, base, mean_ref)
        row = lax.broadcasted_iota(jnp.int32, (UNIT, lats), 0) + base - offset
        valid = jnp.logical_and(row >= 0, row < band)

        def moment(t, carry):
            a = land[t, pl.ds(base, UNIT), :].astype(F32) - center[bins[t]]
            q = a * a
            run2[t] = run2[prev[t]] + q
            run3[t] = run3[prev[t]] + q * a
            square[t] += jnp.where(valid, q, 0.0)
            return carry

        lax.fori_loop(0, steps, moment, 0, unroll=4)
        for source, out in ((run2, second_ref), (run3, third_ref)):
            def close(b, carry, source=source):
                center[b] = source[last[b]] * inverse[b]
                return carry

            lax.fori_loop(0, DAYS, close, 0, unroll=2)
            spread(center, base, out)

    def m_copy(c, start, rows, way):
        half = rows // 2
        if way < len(links):
            k, slot = links[way], links[way] - 1
            source, low, count = mean_ref, start, rows
        elif way == 2:
            k, slot, low, count = 2, 2, start, half
            source = slots.at[0]
        else:
            k, slot, low, count = 1, 2, start + half, rows - half
            source = slots.at[1]
        return pltpu.make_async_remote_copy(
            src_ref=source.at[pl.ds(low, count)],
            dst_ref=slots.at[slot, pl.ds(low, count)],
            send_sem=m_send.at[c, way],
            recv_sem=m_recv.at[c, way],
            device_id={"group": partner(group, k, groups)},
            device_id_type=MESH,
        )

    def family(start, rows):
        owner = [group] + [sender(group, k, groups) for k in range(1, groups)]
        factor = [[hot[f, owner[k]] for k in range(groups)] for f in range(FAM)]

        def one(r, carry):
            at = start + r
            fields = [mean_ref[at].astype(F32)] + [slots[k, at].astype(F32) for k in range(groups - 1)]
            for f in range(FAM):
                total = fields[0] * factor[f][0]
                for k in range(1, groups):
                    total = total + fields[k] * factor[f][k]
                family_ref[f, at] = (total * scale[f]).astype(BF16)
            return carry

        lax.fori_loop(0, rows, one, 0)

    def arrive(c, start, rows):
        for k in range(1, parts):
            z_copy(c, start, rows, k).wait_recv()

    def compute(start, rows):
        lax.fori_loop(
            0, rows // UNIT, lambda u, carry: (unit(pl.multiple_of(start + u * UNIT, UNIT)), carry)[1], 0
        )

    def share(c, start, rows):
        for way in range(len(links)):
            m_copy(c, start, rows, way).start()

    def pass_on(c, start, rows):
        for way in range(len(links)):
            m_copy(c, start, rows, way).wait_recv()
        if relay:
            m_copy(c, start, rows, 2).start()
            m_copy(c, start, rows, 3).start()

    def finish(c, start, rows):
        if relay:
            m_copy(c, start, rows, 2).wait_recv()
            m_copy(c, start, rows, 3).wait_recv()
        family(start, rows)

    count = len(chunks)
    even = sum(rows == CHUNK for _, rows in chunks)

    def step(s):
        if s < count:
            arrive(s, *chunks[s])
            if s + WINDOW < count:
                z_start(s + WINDOW, *chunks[s + WINDOW])
            if s == 0:
                own_copy.wait()
            compute(*chunks[s])
            share(s, *chunks[s])
        if 0 < s <= count:
            pass_on(s - 1, *chunks[s - 1])
        if s >= 2:
            finish(s - 2, *chunks[s - 2])

    def middle(s, carry):
        at = lambda c: (c, pl.multiple_of(c * CHUNK, CHUNK), CHUNK)
        arrive(*at(s))
        z_start(*at(s + WINDOW))
        compute(*at(s)[1:])
        share(*at(s))
        pass_on(*at(s - 1))
        finish(*at(s - 2))
        return carry

    high = max(2, even - WINDOW)
    for s in range(min(2, count)):
        step(s)
    lax.fori_loop(2, high, middle, 0)
    for s in range(high, count):
        step(s)

    lanes = nvec.shape[-1]
    folded = jnp.sum(square[...], axis=1) * weight[...]
    totals = jnp.sum(folded, axis=1, keepdims=True)
    here = lax.broadcasted_iota(jnp.int32, (steps, lanes), 0) == lax.broadcasted_iota(
        jnp.int32, (steps, lanes), 1
    )
    mine = jnp.sum(jnp.where(here, totals, 0.0), axis=0, keepdims=True)
    nvec[0] = mine
    nland[me] = mine

    def n_copy(k):
        return pltpu.make_async_remote_copy(
            src_ref=nvec.at[0], dst_ref=nland.at[me], send_sem=n_send.at[k - 1], recv_sem=n_recv.at[k - 1],
            device_id={"tm": partner(me, k, parts)}, device_id_type=MESH,
        )

    def g_copy(k):
        return pltpu.make_async_remote_copy(
            src_ref=nvec.at[1], dst_ref=gland.at[group], send_sem=g_send.at[k - 1], recv_sem=g_recv.at[k - 1],
            device_id={"group": partner(group, k, groups)}, device_id_type=MESH,
        )

    for k in range(1, parts):
        n_copy(k).start()
    step(count)
    for k in range(1, parts):
        n_copy(k).wait_recv()
    model = nland[0]
    for k in range(1, parts):
        model = model + nland[k]
    nvec[1] = model
    gland[group] = model
    for k in range(1, groups):
        g_copy(k).start()
    step(count + 1)
    for k in range(1, groups):
        g_copy(k).wait_recv()
    norm_ref[...] = gland[...]

    for k in range(1, parts):
        n_copy(k).wait_send()
    for k in range(1, groups):
        g_copy(k).wait_send()
    for c in range(count):
        for k in range(1, parts):
            z_copy(c, *chunks[c], k).wait_send()
        for way in range(len(links) + (2 if relay else 0)):
            m_copy(c, *chunks[c], way).wait_send()


def fused(x, scalars, weight, parts, groups, band, span, chunks):
    own, lons, lats = x.shape
    steps = own * parts
    lanes = -(-steps // 128) * 128
    smem = pl.BlockSpec(memory_space=pltpu.SMEM)
    vmem = pl.BlockSpec(memory_space=pltpu.VMEM)
    ways = 4 if groups == 4 else groups - 1
    dma = pltpu.SemaphoreType.DMA
    wide = -(-lats // 128) * 128
    scratch = [
        ((steps, span, lats), BF16),
        ((groups - 1, span, DAYS, lats), BF16),
        ((steps + 1, UNIT, lats), F32),
        ((steps + 1, UNIT, lats), F32),
        ((steps + 1, UNIT, lats), F32),
        ((DAYS, UNIT, lats), F32),
        ((steps, UNIT, lats), F32),
        ((2, 1, lanes), F32),
        ((parts, 1, lanes), F32),
        ((groups, 1, lanes), F32),
    ]
    size = sum(math.prod(shape[:-1]) * wide * jnp.dtype(kind).itemsize for shape, kind in scratch)
    field = pltpu.VMEM((span, DAYS, lats), BF16)
    return pl.pallas_call(
        functools.partial(fused_kernel, parts, groups, band, lons, chunks),
        in_specs=[smem] * 6 + [vmem, pl.BlockSpec(memory_space=pl.ANY)],
        out_specs=[vmem] * 5,
        out_shape=[field] * 3
        + [pltpu.VMEM((FAM, span, DAYS, lats), BF16), pltpu.VMEM((groups, 1, lanes), F32)],
        scratch_shapes=[pltpu.VMEM(shape, kind) for shape, kind in scratch]
        + [
            dma((1,)),
            dma((len(chunks), parts - 1)),
            dma((len(chunks), parts - 1)),
            dma((len(chunks), ways)),
            dma((len(chunks), ways)),
            dma((parts - 1,)),
            dma((parts - 1,)),
            dma((groups - 1,)),
            dma((groups - 1,)),
        ],
        compiler_params=pltpu.CompilerParams(
            collective_id=0, has_side_effects=True, vmem_limit_bytes=size + 3 * 2**20
        ),
        cost_estimate=pl.CostEstimate(
            flops=20 * steps * span * lats, bytes_accessed=8 * steps * span * lats, transcendentals=0
        ),
    )(*scalars, weight, x)


def place_kernel(steps, offset, total, mean, second, third, family, norm, *refs):
    outs, norm_out, sem = refs[:4], refs[4], refs[5]
    rows = outs[0].shape[0]
    copies = [
        pltpu.make_async_copy(a.at[pl.ds(offset[0], rows)], o, sem.at[i])
        for i, (a, o) in enumerate(zip((mean, second, third), outs))
    ]
    copies += [
        pltpu.make_async_copy(family.at[f, pl.ds(offset[0], rows)], outs[3].at[f], sem.at[3 + f])
        for f in range(family.shape[0])
    ]
    for copy in copies:
        copy.start()
    for g in range(norm.shape[0]):
        norm_out[pl.ds(g, 1), :] = jnp.sqrt(norm[g][:, :steps] / total[0])
    for copy in copies:
        copy.wait()


def place(fields, offset, total, steps, band):
    mean, norm = fields[0], fields[4]
    _, days, lats = mean.shape
    smem = pl.BlockSpec(memory_space=pltpu.SMEM)
    hbm = pl.BlockSpec(memory_space=pl.ANY)
    vmem = pl.BlockSpec(memory_space=pltpu.VMEM)
    out = jax.ShapeDtypeStruct((band, days, lats), BF16)
    return pl.pallas_call(
        functools.partial(place_kernel, steps),
        in_specs=[smem, smem] + [vmem] * 5,
        out_specs=[hbm] * 4 + [vmem],
        out_shape=[out] * 3
        + [
            jax.ShapeDtypeStruct((FAM, band, days, lats), BF16),
            jax.ShapeDtypeStruct((norm.shape[0], steps), F32),
        ],
        scratch_shapes=[pltpu.SemaphoreType.DMA((3 + FAM,))],
        compiler_params=pltpu.CompilerParams(vmem_limit_bytes=2**20),
    )(offset, total, *fields)


def local(parts, groups, precip, day_bins, family_of):
    _, own, lons, lats = precip.shape
    band = lons // parts
    steps = own * parts
    span = -(-(band + max(p * band % UNIT for p in range(parts))) // UNIT) * UNIT
    whole = (span - UNIT) // CHUNK
    chunks = [(c * CHUNK, CHUNK) for c in range(whole)]
    chunks += [(low, UNIT) for low in range(whole * CHUNK, span, UNIT)]

    time = jnp.arange(steps, dtype=jnp.int32)
    days = jnp.arange(DAYS, dtype=jnp.int32)
    onehot = day_bins[None, :] == days[:, None]
    inverse = 1.0 / jnp.maximum(jnp.sum(onehot.astype(F32), axis=1), 1.0)
    last = jnp.max(jnp.where(onehot, time[None, :], -1), axis=1)
    last = jnp.where(last < 0, steps, last)
    before = (day_bins[None, :] == day_bins[:, None]) & (time[None, :] < time[:, None])
    prev = jnp.max(jnp.where(before, time[None, :], -1), axis=1)
    prev = jnp.where(prev < 0, steps, prev)
    hot = (family_of[None, :] == jnp.arange(FAM, dtype=jnp.int32)[:, None]).astype(F32)
    scale = 1.0 / jnp.maximum(jnp.sum(hot, axis=1), 1.0)
    weight = lat_weight(lats)
    total = (lons * jnp.sum(weight)).reshape(1)

    scalars = (day_bins, prev, last, inverse, hot, scale)
    fields = fused(precip[0], scalars, weight[None, :], parts, groups, band, span, chunks)
    me = lax.axis_index("tm")
    offset = (me * band - jnp.minimum(me * band // UNIT * UNIT, lons - span)).reshape(1).astype(jnp.int32)
    mean, second, third, family, norm = place(fields, offset, total, steps, band)
    turned = [jnp.swapaxes(a, 0, 1)[None] for a in (mean, second, third)]
    return (*turned, jnp.swapaxes(family, 1, 2), norm)


def solution(mesh):
    in_specs = (P("group", "tm", None, None), P(), P())
    out_specs = (
        P("group", None, "tm", None),
        P("group", None, "tm", None),
        P("group", None, "tm", None),
        P(None, None, "tm", None),
        P(),
    )
    body = functools.partial(local, mesh.shape["tm"], mesh.shape["group"])
    return jax.shard_map(body, mesh=mesh, in_specs=in_specs, out_specs=out_specs, check_vma=False)
```

time: 403 us -> 253 us (0.63)
  blocking collectives: 200 us -> 0 us
  Pallas kernels: 42 us -> 241 us
  local copies, waits for them, and re-layouts: 83 us -> 0.65 us
  waiting for transfers between devices: 50.7 us -> 0 us
  between operations: 14.7 us -> 1.32 us
  starting transfers between devices: 5.61 us -> 0 us
  other arithmetic: 2.55 us -> 7.37 us
    pallas_call x8 -> x2, Pallas kernels: 42 us -> 241 us  [the longest x1 231 us: fused(): pl.pallas_call(functools.partial(fused_kernel, parts, groups, band, lons,...]
    all_to_all x3 -> x0, blocking collectives: 159 us -> none  [local(): got = lax.all_to_all(sent, 'tm', split_axis=0, concat_axis=0)]
    all_to_all x1 -> x0, waiting for transfers between devices: 50.7 us -> none  [local(): got = lax.all_to_all(sent, 'tm', split_axis=0, concat_axis=0)]
    unnamed x66 -> x2, local copies, waits for them, and re-layouts: 50.6 us -> 0.65 us
    psum x1 -> x0, blocking collectives: 40.7 us -> none  [local(): anomaly_norm = jnp.sqrt(lax.psum(placed, ('group', 'tm')) / total_weight)]
    reshape x1 -> x0, local copies, waits for them, and re-layouts: 12.5 us -> none  [local(): banded = precip.reshape(own, parts, band, lats)]
    transpose x3 -> x0, local copies, waits for them, and re-layouts: 9.18 us -> none  [local(): sent = jnp.transpose(banded[:, :, low:high], (1, 0, 2, 3))]
    optimization_barrier x4 -> x0, local copies, waits for them, and re-layouts: 6.48 us -> none  [the longest x2 3.38 us: local(): lax.optimization_barrier((sent, got, gathered[k - 2]))]
  transfers between devices with their start and end apart: 5 -> 0, of which waited for: 1 -> 0; matrix products, arithmetic and copies ran while one was open for 5% -> 0% of each run, Pallas kernels for 8% -> 0%
where the time goes in v1:
time: 253 us; the launch traced here: 250 us
  Pallas kernels  241 us (95%)
  other arithmetic  7.37 us (3%)
    pallas_call x1, Pallas kernels, fused(): pl.pallas_call(functools.partial(fused_kernel, parts, groups, band, lons,...  231 us
    pallas_call x1, Pallas kernels, place(): pl.pallas_call(functools.partial(place_kernel, steps), in_specs=[smem, sm...  9.5 us

profile of v1, /device:TPU:17, one launch (start us, length us, event | category | flops | bytes accessed | tf_op | source)
XLA Modules:
  0.0 249.9 jit_solution(558494751630126261)
XLA Ops:
  0.6 0.7 cosine_reduce_fusion
  2.0 0.8 fusion.2
  2.7 0.5 maximum_divide_fusion.scale
  3.2 0.8 convert_reduce_fusion
  4.0 0.5 maximum_divide_fusion.1.inverse
  4.5 0.9 select_reduce_fusion
  5.5 0.8 select_reduce_fusion.1
  6.2 0.5 compare_select_fusion.last
  6.8 1.2 fusion.1.hot
  8.0 0.7 multiply_cosine_fusion.weight
  8.7 0.0 copy-start
  8.7 0.7 copy-done
  9.3 231.1 %shard_map.74 = (bf16[184,16,720]{2,1,0:T(8,128)(2,1)S(1)}, bf16[184,16,720]{2,1,0:T(8,128)(2,1)S(1)}, bf16[184,16,720]{2,1,0:T(8,128)(2,1)S(1)}, bf16[3,184,16,720]{3,2,1,0:T(8,128)(2,1)S(1)}, f32[4,1,128]{2,1,0:T(1,128)S(1)}) custom-call(s32[32]{0:T(128)S(1)} %copy-done, s32[32]{0:T(128)S(1)} %compare_select_fusion.1.prev, s32[16]{0:T(128)} %compare_select_fusion.last, ...), custom_call_target="tpu_custom_call" | custom-call | flops 84787200 | bytes 33914880 | tf_op jit(solution)/shard_map/pallas_call | solution.py:304
  240.4 9.5 %shard_map.75 = (bf16[180,16,720]{2,1,0:T(8,128)(2,1)}, bf16[180,16,720]{2,1,0:T(8,128)(2,1)}, bf16[180,16,720]{2,1,0:T(8,128)(2,1)}, bf16[3,180,16,720]{3,2,1,0:T(8,128)(2,1)}, f32[4,32]{1,0:T(4,128)}) custom-call(s32[1]{0:T(128)} %bitcast.offset, f32[1]{0:T(128)} %bitcast.1.total, bf16[184,16,720]{2,1,0:T(8,128)(2,1)S(1)} %get-tuple-element.15.mean, ...), custom_call_target="tpu_custom_call" | custom-call | tf_op jit(solution)/shard_map/pallas_call | solution.py:357
  (1 shorter events, 0.0 us)
Async XLA Ops:
  8.7 0.7 copy-start
